TPU v7x, 32 devices: a whole 2x2x4 slice. The times are simulated.
32 devices in a mesh: grp: 2 (over y), bn: 16 (over z, x, core).
Axes of the slice: x: 2, y: 2, z: 4, core: 2. Of those that a mesh axis runs over, the one named last changes fastest.
Arguments:
- images: bfloat16 [32, 19, 19, 384], P(('grp', 'bn')), parts along dimension 0, may hold values from -56 to 56
- expand_weight: bfloat16 [384, 2304], P('bn'), may hold values from -0.3125 to 0.3125
- expand_gain: float32 [2304], replicated, may hold values from 0.5 to 2
- expand_shift: float32 [2304], replicated, may hold values from -3 to 3
- depth_weight: bfloat16 [25, 2304], replicated, may hold values from -1.25 to 1.25
- depth_gain: float32 [2304], replicated, may hold values from 0.5 to 2
- depth_shift: float32 [2304], replicated, may hold values from -3 to 3
- squeeze_weight: bfloat16 [2304, 96], replicated, may hold values from -0.125 to 0.125
- squeeze_bias: float32 [96], replicated, may hold values from -4 to 4
- excite_weight: bfloat16 [96, 2304], replicated, may hold values from -0.625 to 0.625
- excite_bias: float32 [2304], replicated, may hold values from -4 to 4
- project_weight: bfloat16 [2304, 384], P('bn'), may hold values from -0.125 to 0.125
- project_gain: float32 [384], replicated, may hold values from 0.5 to 2
- project_shift: float32 [384], replicated, may hold values from -3 to 3
- group_table: int32 [32], P('grp'), parts along dimension 0, may hold values from 0 to 1, as said below
Outputs:
- block_output: bfloat16 [32, 19, 19, 384], P(('grp', 'bn')), parts along dimension 0
There are 2 independent parts, one for each index of `grp`. A program takes and returns all parts, laid end to end along the dimension named above; an argument that names none is the same for every part. Nothing has to cross between parts.
Inputs may be any that keep to these rules, and one draw needn't show every extreme that they name: `group_table`: each of the 2 statistics groups holds at least 4 images, placed anywhere among the images.
All inputs are finite; a program needn't handle non-finite values.
Results may differ from a plain program's by a relative error of at most 0.0065.
Values may be sent and summed in bfloat16 or wider, within the bound.
A program may use at most 64 MiB of HBM per device.

v0:
```python
import jax
import jax.numpy as jnp
from jax import lax
from jax.sharding import PartitionSpec as P

KERNEL = 5
STAT_GROUPS = 2
epsilon = 0.001


def normalize(values, centre, inverse, gain, shift):
    return (values.astype(jnp.float32) - centre) * inverse * gain + shift


def depthwise(widened, depth_weight, height, breadth):
    spatial = widened.reshape(height, breadth, widened.shape[-1])
    margin = KERNEL // 2
    padded = jnp.pad(spatial, ((margin, margin), (margin, margin), (0, 0)))
    accumulated = jnp.zeros(spatial.shape, jnp.float32)
    for row_shift in range(KERNEL):
        for col_shift in range(KERNEL):
            window = padded[row_shift : row_shift + height, col_shift : col_shift + breadth]
            accumulated = accumulated + window.astype(jnp.float32) * depth_weight[
                row_shift * KERNEL + col_shift
            ].astype(jnp.float32)
    return accumulated.reshape(height * breadth, spatial.shape[-1]).astype(jnp.bfloat16)


def group_moments(values, selector, population):
    totals = jnp.sum(values, axis=0, dtype=jnp.float32)
    squares = jnp.sum(jnp.square(values.astype(jnp.float32)), axis=0)
    weighted = selector[:, None, None] * jnp.stack([totals, squares])[None]
    summed = lax.psum(weighted, "bn")
    picked = jnp.sum(selector[:, None, None] * summed, axis=0)
    centre = picked[0] / population
    spread = picked[1] / population - centre * centre
    return (centre, lax.rsqrt(spread + epsilon))


def on_device(
    images,
    expand_weight,
    expand_gain,
    expand_shift,
    depth_weight,
    depth_gain,
    depth_shift,
    squeeze_weight,
    squeeze_bias,
    excite_weight,
    excite_bias,
    project_weight,
    project_gain,
    project_shift,
    group_table,
):
    height, breadth, channels = (images.shape[1], images.shape[2], images.shape[3])
    pixels = height * breadth
    flattened = images.reshape(pixels, channels)
    device_rank = lax.axis_index("bn")
    ranks_all = jnp.arange(group_table.shape[0], dtype=jnp.int32)
    my_group = jnp.sum(jnp.where(ranks_all == device_rank, group_table, 0))
    members = jnp.sum((group_table == my_group).astype(jnp.float32))
    population = members * pixels
    selector = (jnp.arange(STAT_GROUPS, dtype=jnp.int32) == my_group).astype(jnp.float32)
    inputs = flattened
    expanded = jnp.dot(
        inputs,
        lax.all_gather(expand_weight, "bn", axis=0, tiled=True),
        preferred_element_type=jnp.float32,
    ).astype(jnp.bfloat16)
    centre, inverse = group_moments(expanded, selector, population)
    widened = jax.nn.silu(normalize(expanded, centre, inverse, expand_gain, expand_shift)).astype(
        jnp.bfloat16
    )
    filtered = depthwise(widened, depth_weight, height, breadth)
    centre, inverse = group_moments(filtered, selector, population)
    activated = jax.nn.silu(normalize(filtered, centre, inverse, depth_gain, depth_shift)).astype(
        jnp.bfloat16
    )
    pooled = (jnp.sum(activated, axis=0, dtype=jnp.float32) / pixels).astype(jnp.bfloat16)[None, :]
    squeezed = jax.nn.silu(
        jnp.dot(pooled, squeeze_weight, preferred_element_type=jnp.float32) + squeeze_bias
    ).astype(jnp.bfloat16)
    excitation = jax.nn.sigmoid(
        jnp.dot(squeezed, excite_weight, preferred_element_type=jnp.float32) + excite_bias
    )
    gated_input = (activated * excitation).astype(jnp.bfloat16)
    inputs = gated_input
    projected = jnp.dot(
        inputs,
        lax.all_gather(project_weight, "bn", axis=0, tiled=True),
        preferred_element_type=jnp.float32,
    ).astype(jnp.bfloat16)
    centre, inverse = group_moments(projected, selector, population)
    output = flattened.astype(jnp.float32) + normalize(
        projected, centre, inverse, project_gain, project_shift
    )
    return output.astype(jnp.bfloat16).reshape(images.shape)


def solution(mesh):
    return jax.shard_map(
        on_device,
        mesh=mesh,
        in_specs=(
            P(("grp", "bn"), None, None, None),
            P("bn", None),
            P(),
            P(),
            P(),
            P(),
            P(),
            P(),
            P(),
            P(),
            P(),
            P("bn", None),
            P(),
            P(),
            P("grp"),
        ),
        out_specs=P(("grp", "bn"), None, None, None),
        check_vma=False,
    )
```

profile of v0, /device:TPU:0, one launch (start us, length us, event | category | flops | bytes accessed | tf_op | source)
XLA Modules:
  0.0 257.8 jit_solution(15007953222312947867)
XLA Ops:
  6.5 0.0 copy-start
  6.5 0.0 all-gather.3.cloned.1.call-start
  6.5 0.7 all-gather.3.cloned.1.call-update
  7.3 0.0 all-gather.5.cloned.1.call-start
  7.3 0.7 all-gather.5.cloned.1.call-update
  8.0 1.3 fusion.15
  9.3 0.6 compare_convert_fusion.1
  10.0 1.9 fusion.16
  11.9 1.9 convert_reduce_fusion.27
  13.7 1.1 convert_reduce_fusion.26
  14.9 1.1 reshape.239
  16.5 0.0 copy-start.2
  16.5 0.0 copy-start.3
  16.6 36.0 %all-gather.3.cloned.1.call-done = bf16[384,2304]{1,0:T(8,128)(2,1)} async-done(((bf16[24,2304]{1,0:T(8,128)(2,1)}), bf16[384,2304]{1,0:T(8,128)(2,1)}) %all-gather.3.cloned.1.call-update) | async-done | bytes 1769488 | tf_op jit(solution)/shard_map/all_gather | solution.py:69
  52.5 3.7 %convert_reduce_fusion = (f32[2304]{0:T(1024)S(1)}, f32[2304]{0:T(1024)S(1)}, bf16[361,2304]{1,0:T(8,128)(2,1)}) fusion(bf16[361,384]{1,0:T(8,128)(2,1)S(1)} %reshape.239, bf16[384,2304]{1,0:T(8,128)(2,1)} %all-gather.3.cloned.1.call-done), kind=kOutput, calls=%fused_computation.2 | convolution fusion | flops 642933504 | bytes 3728640 | tf_op jit(solution)/shard_map/dot_general | solution.py:67
  56.3 0.1 broadcast_multiply_fusion.1
  56.4 59.8 %psum.21 = f32[2,2,2304]{2,1,0:T(2,128)S(1)} all-reduce(f32[2,2,2304]{2,1,0:T(2,128)S(1)} %broadcast_multiply_fusion.1), channel_id=1, replica_groups=mesh['grp'=2,'bn'=16] {'bn'}, use_global_device_ids=true, to_apply=%region_3.4 | all-reduce | flops 9216 | bytes 73728 | tf_op jit(solution)/shard_map/psum | solution.py:33
  116.2 0.1 multiply_reduce_fusion.3
  116.3 0.1 fusion.26
  116.3 0.0 copy-done.2
  116.4 0.0 copy-done.3
  116.4 2.6 %fusion.9 = bf16[361,2304]{1,0:T(8,128)(2,1)S(1)} fusion(bf16[361,2304]{1,0:T(8,128)(2,1)} %get-tuple-element.43, f32[2304]{0:T(1024)S(1)} %copy-done.2, f32[2304]{0:T(1024)S(1)} %copy-done.3, f32[2304]{0:T(1024)S(1)} %get-tuple-element.39, f32[2304]{0:T(1024)S(1)} %get-tuple-element.38), kind=kLoop, calls=%fused_computation.17 | loop fusion | flops 8317440 | bytes 3363840 | tf_op jit(solution)/shard_map/convert_element_type | solution.py:73
  119.0 2.0 reshape.240
  121.0 32.3 %convert_reduce_fusion.2 = (f32[2304]{0:T(1024)S(1)}, f32[2304]{0:T(1024)S(1)}, bf16[19,19,2304]{2,1,0:T(8,128)(2,1)S(1)}) fusion(f32[2304]{0:T(1024)S(1)} %get-tuple-element.34, f32[2304]{0:T(1024)S(1)} %get-tuple-element.35, f32[2304]{0:T(1024)S(1)} %get-tuple-element.12, f32[2304]{0:T(1024)S(1)} %get-tuple-element.13, f32[2304]{0:T(1024)S(1)} %get-tuple-element.14, ...), kind=kLoop, calls=%fused_computation.20 | loop fusion | flops 65703168 | bytes 3575808 | tf_op jit(solution)/shard_map/reduce_sum | solution.py:30
  153.3 0.0 copy-start.4
  153.3 0.0 copy-start.5
  153.3 0.0 copy-start.1
  153.3 0.0 copy-start.9
  153.4 0.0 copy-start.6
  153.4 2.2 reshape.267
  155.6 0.1 broadcast_multiply_fusion
  155.7 57.9 %psum.22 = f32[2,2,2304]{2,1,0:T(2,128)S(1)} all-reduce(f32[2,2,2304]{2,1,0:T(2,128)S(1)} %broadcast_multiply_fusion), channel_id=1, replica_groups=mesh['grp'=2,'bn'=16] {'bn'}, use_global_device_ids=true, to_apply=%region_8.9 | all-reduce | flops 9216 | bytes 73728 | tf_op jit(solution)/shard_map/psum | solution.py:33
  213.6 0.1 multiply_reduce_fusion.2
  213.7 0.1 fusion.25
  213.7 0.0 copy-done.4
  213.7 0.0 copy-done.5
  213.8 1.6 convert_reduce_fusion.1
  215.3 0.0 copy-done
  215.3 0.0 copy-done.1
  215.4 0.0 copy-done.9
  215.4 0.4 convolution_reduce_fusion
  215.8 0.0 copy-done.6
  215.8 0.0 copy-start.7
  215.8 0.0 copy-start.8
  215.9 0.0 all-gather.5.cloned.1.call-done
  215.9 3.9 %fusion.24 = (f32[384]{0:T(512)S(1)}, f32[384]{0:T(512)S(1)}, f32[361,384]{1,0:T(8,128)S(1)}) fusion(bf16[2304,384]{1,0:T(8,128)(2,1)} %all-gather.5.cloned.1.call-done, f32[2304]{0:T(1024)S(1)} %add_divide_fusion, f32[2304]{0:T(1024)S(1)} %copy-done.4, f32[2304]{0:T(1024)S(1)} %copy-done.5, f32[2304]{0:T(1024)S(1)} %get-tuple-element.37, ...), kind=kOutput, calls=%fused_computation.106 | convolution fusion | flops 649452672 | bytes 5700096 | tf_op jit(solution)/shard_map/dot_general | solution.py:90
  219.8 0.1 broadcast_multiply_fusion.2
  219.9 30.0 %psum.23 = f32[2,2,384]{2,1,0:T(2,128)S(1)} all-reduce(f32[2,2,384]{2,1,0:T(2,128)S(1)} %broadcast_multiply_fusion.2), channel_id=1, replica_groups=mesh['grp'=2,'bn'=16] {'bn'}, use_global_device_ids=true, to_apply=%region_13.14 | all-reduce | flops 1536 | bytes 12288 | tf_op jit(solution)/shard_map/psum | solution.py:33
  249.9 0.1 multiply_reduce_fusion.4
  250.0 0.0 copy-done.7
  250.0 0.0 copy-done.8
  250.0 0.1 add_convert_fusion.1
  250.2 0.8 reshape.241
  (13 shorter events, 0.2 us)
Async XLA Ops:
  6.5 208.8 %copy-start = (bf16[96,2304]{1,0:T(8,128)(2,1)S(1)}, bf16[96,2304]{1,0:T(8,128)(2,1)}, u32[]{:S(2)}) copy-start(bf16[96,2304]{1,0:T(8,128)(2,1)} %param.24) | copy-start | bytes 1327108
  6.5 46.0 %all-gather.3.cloned.1.call-start = ((), (), s32[]{:S(2)}) async-start(), calls=%async_computation | async-start | bytes 1880064 | tf_op jit(solution)/shard_map/all_gather | solution.py:69
  7.3 208.6 %all-gather.5.cloned.1.call-start = ((), (), s32[]{:S(2)}) async-start(), calls=%async_computation.1 | async-start | bytes 1880064 | tf_op jit(solution)/shard_map/all_gather | solution.py:92
  16.5 99.8 %copy-start.2 = (f32[2304]{0:T(1024)S(1)}, f32[2304]{0:T(1024)}, u32[]{:S(2)}) copy-start(f32[2304]{0:T(1024)} %param.18) | copy-start | bytes 27652
  16.5 99.8 %copy-start.3 = (f32[2304]{0:T(1024)S(1)}, f32[2304]{0:T(1024)}, u32[]{:S(2)}) copy-start(f32[2304]{0:T(1024)} %param.17) | copy-start | bytes 27652
  153.3 60.4 %copy-start.4 = (f32[2304]{0:T(1024)S(1)}, f32[2304]{0:T(1024)}, u32[]{:S(2)}) copy-start(f32[2304]{0:T(1024)} %param.21) | copy-start | bytes 27652
  153.3 60.4 %copy-start.5 = (f32[2304]{0:T(1024)S(1)}, f32[2304]{0:T(1024)}, u32[]{:S(2)}) copy-start(f32[2304]{0:T(1024)} %param.20) | copy-start | bytes 27652
  153.3 62.0 %copy-start.1 = (bf16[2304,96]{0,1:T(8,128)(2,1)S(1)}, bf16[2304,96]{0,1:T(8,128)(2,1)}, u32[]{:S(2)}) copy-start(bf16[2304,96]{0,1:T(8,128)(2,1)} %param.22) | copy-start | bytes 1327108
  153.3 62.0 %copy-start.9 = (f32[96]{0:T(128)S(1)}, f32[96]{0:T(128)}, u32[]{:S(2)}) copy-start(f32[96]{0:T(128)} %param.23) | copy-start | bytes 1156
  153.4 62.5 %copy-start.6 = (f32[2304]{0:T(1024)S(1)}, f32[2304]{0:T(1024)}, u32[]{:S(2)}) copy-start(f32[2304]{0:T(1024)} %param.25) | copy-start | bytes 27652
  215.8 34.2 %copy-start.7 = (f32[384]{0:T(512)S(1)}, f32[384]{0:T(512)}, u32[]{:S(2)}) copy-start(f32[384]{0:T(512)} %param.28) | copy-start | bytes 4612
  215.8 34.2 %copy-start.8 = (f32[384]{0:T(512)S(1)}, f32[384]{0:T(512)}, u32[]{:S(2)}) copy-start(f32[384]{0:T(512)} %param.27) | copy-start | bytes 4612
Sparse Core Ops, SparseCore 0:
  9.5 42.9 all-gather.2
  54.7 39.2 all-gather.4
where the time goes:
time: 258 us
  blocking collectives  148 us (57%)
  other arithmetic  44.2 us (17%)
  waiting for transfers between devices  37.4 us (14%)
  between operations  14.3 us (6%)
  matrix products  8.06 us (3%)
  local copies, waits for them, and re-layouts  6.24 us (2%)
    psum x3, blocking collectives, group_moments(): summed = lax.psum(weighted, 'bn')  148 us
    all_gather x1, waiting for transfers between devices, on_device(): lax.all_gather(expand_weight, 'bn', axis=0, tiled=True)  36 us
    reduce_sum x1, other arithmetic, group_moments(): totals = jnp.sum(values, axis=0, dtype=jnp.float32)  32.3 us
  transfers between devices with their start and end apart: 2, of which 1 were waited for; matrix products, arithmetic and copies ran while one was open for 21% of the time, Pallas kernels for 0%

commit v1 on v0

--- a/solution.py
+++ b/solution.py
@@ -1,3 +1,4 @@
+import functools
 import jax
 import jax.numpy as jnp
 from jax import lax
@@ -6,6 +7,18 @@
 KERNEL = 5
 STAT_GROUPS = 2
 epsilon = 0.001
+
+
+def define_stops_all_here(buf, across):
+    full_n = jax.lax.psum(1, across)
+    b_next = buf
+    current_block = lambda h_now: [(h, h ^ h_now) for h in range(full_n)]
+    for kk in range(full_n.bit_length() - 1):
+        b_next = b_next + jax.lax.ppermute(b_next, across, current_block(1 << kk))
+    return b_next
+
+
+enter_values = functools.partial(define_stops_all_here, across="bn")
 
 
 def normalize(values, centre, inverse, gain, shift):
@@ -30,7 +43,7 @@
     totals = jnp.sum(values, axis=0, dtype=jnp.float32)
     squares = jnp.sum(jnp.square(values.astype(jnp.float32)), axis=0)
     weighted = selector[:, None, None] * jnp.stack([totals, squares])[None]
-    summed = lax.psum(weighted, "bn")
+    summed = enter_values(weighted)
     picked = jnp.sum(selector[:, None, None] * summed, axis=0)
     centre = picked[0] / population
     spread = picked[1] / population - centre * centre

time: 258 us -> 150 us (0.58)
  blocking collectives: 148 us -> 0 us
  waiting for transfers between devices: 37.4 us -> 77.2 us
  starting transfers between devices: 0.04 us -> 3.46 us
  other arithmetic: 44.2 us -> 40.9 us
    psum x3 -> x0, blocking collectives: 148 us -> none  [group_moments(): summed = lax.psum(weighted, 'bn')]
    ppermute x0 -> x12, waiting for transfers between devices: none -> 34.3 us  [define_stops_all_here(): b_next = b_next + jax.lax.ppermute(b_next, across, current_block(1 << kk))]
    all_gather x1, waiting for transfers between devices: 36 us -> 42.1 us  [on_device(): lax.all_gather(expand_weight, 'bn', axis=0, tiled=True)]
    ppermute x0 -> x12, starting transfers between devices: none -> 3.41 us  [define_stops_all_here(): b_next = b_next + jax.lax.ppermute(b_next, across, current_block(1 << kk))]
  transfers between devices with their start and end apart: 2 -> 14, of which waited for: 1 -> 13; matrix products, arithmetic and copies ran while one was open for 21% -> 31% of each run, Pallas kernels for 0% -> 0%
where the time goes in v1:
time: 150 us
  waiting for transfers between devices  77.2 us (51%)
  other arithmetic  40.9 us (27%)
  between operations  14.3 us (10%)
  matrix products  8.03 us (5%)
  local copies, waits for them, and re-layouts  6.43 us (4%)
  starting transfers between devices  3.46 us (2%)
    all_gather x1, waiting for transfers between devices, on_device(): lax.all_gather(expand_weight, 'bn', axis=0, tiled=True)  42.1 us
    ppermute x12, waiting for transfers between devices, define_stops_all_here(): b_next = b_next + jax.lax.ppermute(b_next, across, current_block(1 << kk))  34.3 us
    reduce_sum x1, other arithmetic, group_moments(): totals = jnp.sum(values, axis=0, dtype=jnp.float32)  31.5 us
    dot_general x1, matrix products, on_device(): jnp.dot(inputs, lax.all_gather(project_weight, 'bn', axis=0, tiled=True),...  3.9 us
    dot_general x1, matrix products, on_device(): jnp.dot(inputs, lax.all_gather(expand_weight, 'bn', axis=0, tiled=True),...  3.71 us
    ppermute x12, starting transfers between devices, define_stops_all_here(): b_next = b_next + jax.lax.ppermute(b_next, across, current_block(1 << kk))  3.41 us
  transfers between devices with their start and end apart: 14, of which 13 were waited for; matrix products, arithmetic and copies ran while one was open for 31% of the time, Pallas kernels for 0%

profile of v1, /device:TPU:0, one launch (start us, length us, event | category | flops | bytes accessed | tf_op | source)
XLA Modules:
  0.0 150.3 jit_solution(4046373924541120378)
XLA Ops:
  6.5 0.7 all-gather.3.cloned.1.call-update
  7.3 0.0 all-gather.5.cloned.1.call-start
  7.3 1.1 reshape.239
  8.4 1.3 fusion.15
  9.7 0.6 compare_convert_fusion.1
  10.3 0.0 copy-start.2
  10.4 0.0 copy-start.11
  10.4 0.0 copy-start.3
  10.4 0.0 copy-start.4
  10.4 42.1 %all-gather.3.cloned.1.call-done = bf16[384,2304]{1,0:T(8,128)(2,1)} async-done(((bf16[24,2304]{1,0:T(8,128)(2,1)}), bf16[384,2304]{1,0:T(8,128)(2,1)}) %all-gather.3.cloned.1.call-update) | async-done | bytes 1769488 | tf_op jit(solution)/shard_map/all_gather | solution.py:82
  52.5 3.7 %convert_reduce_fusion = (f32[2304]{0:T(1024)S(1)}, f32[2304]{0:T(1024)S(1)}, bf16[361,2304]{1,0:T(8,128)(2,1)}) fusion(bf16[361,384]{1,0:T(8,128)(2,1)S(1)} %reshape.239, bf16[384,2304]{1,0:T(8,128)(2,1)} %all-gather.3.cloned.1.call-done), kind=kOutput, calls=%fused_computation.2 | convolution fusion | flops 642933504 | bytes 3728640 | tf_op jit(solution)/shard_map/dot_general | solution.py:80
  56.3 0.1 broadcast_multiply_fusion.1
  56.4 0.3 collective-permute-start
  56.7 0.0 all-gather.5.cloned.1.call-update
  56.7 1.0 collective-permute-done
  57.6 0.1 fusion.25
  57.7 0.6 collective-permute-start.1
  58.4 0.5 convert_reduce_fusion.27
  58.8 2.9 %collective-permute-done.1 = f32[2,2,2304]{2,1,0:T(2,128)S(1)} collective-permute-done((f32[2,2,2304]{2,1,0:T(2,128)S(1)}, f32[2,2,2304]{2,1,0:T(2,128)S(1)}, u32[]{:S(2)}, u32[]{:S(2)}) %collective-permute-start.1) | collective-permute-done | bytes 36896 | tf_op jit(solution)/shard_map/ppermute | solution.py:17
  61.8 0.1 fusion.39
  61.8 0.5 collective-permute-start.2
  62.3 0.2 convert_reduce_fusion.26
  62.5 3.4 %collective-permute-done.2 = f32[2,2,2304]{2,1,0:T(2,128)S(1)} collective-permute-done((f32[2,2,2304]{2,1,0:T(2,128)S(1)}, f32[2,2,2304]{2,1,0:T(2,128)S(1)}, u32[]{:S(2)}, u32[]{:S(2)}) %collective-permute-start.2) | collective-permute-done | bytes 36896 | tf_op jit(solution)/shard_map/ppermute | solution.py:17
  65.9 0.7 collective-permute-start.3
  66.6 1.2 fusion.16
  68.5 3.3 %collective-permute-done.3 = f32[2,2,2304]{2,1,0:T(2,128)S(1)} collective-permute-done((f32[2,2,2304]{2,1,0:T(2,128)S(1)}, f32[2,2,2304]{2,1,0:T(2,128)S(1)}, u32[]{:S(2)}, u32[]{:S(2)}) %collective-permute-start.3) | collective-permute-done | bytes 36896 | tf_op jit(solution)/shard_map/ppermute | solution.py:17
  71.8 0.1 multiply_reduce_fusion.3
  71.9 0.1 fusion.29
  72.0 2.6 %fusion.9 = bf16[361,2304]{1,0:T(8,128)(2,1)S(1)} fusion(bf16[361,2304]{1,0:T(8,128)(2,1)} %get-tuple-element.43, f32[2304]{0:T(1024)S(1)} %copy-done.3, f32[2304]{0:T(1024)S(1)} %copy-done.4, f32[2304]{0:T(1024)S(1)} %get-tuple-element.39, f32[2304]{0:T(1024)S(1)} %get-tuple-element.38), kind=kLoop, calls=%fused_computation.17 | loop fusion | flops 8317440 | bytes 3363840 | tf_op jit(solution)/shard_map/convert_element_type | solution.py:86
  74.6 2.2 %reshape.240 = bf16[19,19,2304]{2,1,0:T(8,128)(2,1)} reshape(bf16[361,2304]{1,0:T(8,128)(2,1)S(1)} %fusion.9) | data formatting | bytes 3326976 | tf_op jit(solution)/shard_map/reshape | solution.py:29
  76.8 31.5 %convert_reduce_fusion.2 = (f32[2304]{0:T(1024)S(1)}, f32[2304]{0:T(1024)S(1)}, bf16[19,19,2304]{2,1,0:T(8,128)(2,1)S(1)}) fusion(f32[2304]{0:T(1024)S(1)} %get-tuple-element.34, f32[2304]{0:T(1024)S(1)} %get-tuple-element.35, f32[2304]{0:T(1024)S(1)} %get-tuple-element.12, f32[2304]{0:T(1024)S(1)} %get-tuple-element.13, f32[2304]{0:T(1024)S(1)} %get-tuple-element.14, ...), kind=kLoop, calls=%fused_computation.20 | loop fusion | flops 65703168 | bytes 3575808 | tf_op jit(solution)/shard_map/reduce_sum | solution.py:43
  108.3 0.1 broadcast_multiply_fusion
  108.4 0.1 collective-permute-start.4
  108.5 1.2 collective-permute-done.4
  109.7 0.1 fusion.26
  109.8 0.3 collective-permute-start.5
  110.1 3.7 %collective-permute-done.5 = f32[2,2,2304]{2,1,0:T(2,128)S(1)} collective-permute-done((f32[2,2,2304]{2,1,0:T(2,128)S(1)}, f32[2,2,2304]{2,1,0:T(2,128)S(1)}, u32[]{:S(2)}, u32[]{:S(2)}) %collective-permute-start.5) | collective-permute-done | bytes 36896 | tf_op jit(solution)/shard_map/ppermute | solution.py:17
  113.8 0.1 fusion.38
  113.9 0.1 collective-permute-start.6
  114.0 3.9 %collective-permute-done.6 = f32[2,2,2304]{2,1,0:T(2,128)S(1)} collective-permute-done((f32[2,2,2304]{2,1,0:T(2,128)S(1)}, f32[2,2,2304]{2,1,0:T(2,128)S(1)}, u32[]{:S(2)}, u32[]{:S(2)}) %collective-permute-start.6) | collective-permute-done | bytes 36896 | tf_op jit(solution)/shard_map/ppermute | solution.py:17
  118.0 0.1 collective-permute-start.7
  118.1 2.2 %reshape.267 = f32[361,2304]{1,0:T(8,128)} reshape(bf16[19,19,2304]{2,1,0:T(8,128)(2,1)S(1)} %get-tuple-element.42) | data formatting | bytes 4990464 | tf_op jit(solution)/shard_map/convert_element_type | solution.py:25
  120.3 2.6 %collective-permute-done.7 = f32[2,2,2304]{2,1,0:T(2,128)S(1)} collective-permute-done((f32[2,2,2304]{2,1,0:T(2,128)S(1)}, f32[2,2,2304]{2,1,0:T(2,128)S(1)}, u32[]{:S(2)}, u32[]{:S(2)}) %collective-permute-start.7) | collective-permute-done | bytes 36896 | tf_op jit(solution)/shard_map/ppermute | solution.py:17
  122.9 0.1 multiply_reduce_fusion.2
  123.0 0.1 fusion.28
  123.1 1.6 %convert_reduce_fusion.1 = f32[2304]{0:T(1024)S(1)} fusion(f32[2304]{0:T(1024)S(1)} %copy-done.5, f32[2304]{0:T(1024)S(1)} %copy-done.6, f32[2304]{0:T(1024)S(1)} %get-tuple-element.37, f32[2304]{0:T(1024)S(1)} %get-tuple-element.36, bf16[19,19,2304]{2,1,0:T(8,128)(2,1)S(1)} %get-tuple-element.42), kind=kLoop, calls=%fused_computation.3 | loop fusion | flops 9978624 | bytes 1709568 | tf_op jit(solution)/shard_map/reduce_sum | solution.py:94
  124.7 0.4 convolution_reduce_fusion
  125.1 0.0 copy-start.9
  125.2 0.0 all-gather.5.cloned.1.call-done
  125.2 3.9 %fusion.27 = (f32[384]{0:T(512)S(1)}, f32[384]{0:T(512)S(1)}, f32[361,384]{1,0:T(8,128)S(1)}) fusion(bf16[2304,384]{1,0:T(8,128)(2,1)} %all-gather.5.cloned.1.call-done, f32[2304]{0:T(1024)S(1)} %add_divide_fusion, f32[2304]{0:T(1024)S(1)} %copy-done.5, f32[2304]{0:T(1024)S(1)} %copy-done.6, f32[2304]{0:T(1024)S(1)} %get-tuple-element.37, ...), kind=kOutput, calls=%fused_computation.109 | convolution fusion | flops 649452672 | bytes 5700096 | tf_op jit(solution)/shard_map/dot_general | solution.py:103
  129.1 0.1 broadcast_multiply_fusion.2
  129.2 0.0 collective-permute-start.8
  129.2 1.2 collective-permute-done.8
  130.4 0.1 fusion.24
  130.5 0.4 collective-permute-start.9
  130.8 3.3 %collective-permute-done.9 = f32[2,2,384]{2,1,0:T(2,128)S(1)} collective-permute-done((f32[2,2,384]{2,1,0:T(2,128)S(1)}, f32[2,2,384]{2,1,0:T(2,128)S(1)}, u32[]{:S(2)}, u32[]{:S(2)}) %collective-permute-start.9) | collective-permute-done | bytes 6176 | tf_op jit(solution)/shard_map/ppermute | solution.py:17
  134.1 0.1 fusion.37
  134.2 0.0 collective-permute-start.10
  134.2 3.6 %collective-permute-done.10 = f32[2,2,384]{2,1,0:T(2,128)S(1)} collective-permute-done((f32[2,2,384]{2,1,0:T(2,128)S(1)}, f32[2,2,384]{2,1,0:T(2,128)S(1)}, u32[]{:S(2)}, u32[]{:S(2)}) %collective-permute-start.10) | collective-permute-done | bytes 6176 | tf_op jit(solution)/shard_map/ppermute | solution.py:17
  137.8 0.3 collective-permute-start.11
  138.1 4.2 %collective-permute-done.11 = f32[2,2,384]{2,1,0:T(2,128)S(1)} collective-permute-done((f32[2,2,384]{2,1,0:T(2,128)S(1)}, f32[2,2,384]{2,1,0:T(2,128)S(1)}, u32[]{:S(2)}, u32[]{:S(2)}) %collective-permute-start.11) | collective-permute-done | bytes 6176 | tf_op jit(solution)/shard_map/ppermute | solution.py:17
  142.3 0.1 multiply_reduce_fusion.4
  142.5 0.1 add_convert_fusion.1
  142.6 0.8 reshape.241
  (36 shorter events, 0.2 us)
Async XLA Ops:
  6.5 118.1 %copy-start = (bf16[96,2304]{1,0:T(8,128)(2,1)S(1)}, bf16[96,2304]{1,0:T(8,128)(2,1)}, u32[]{:S(2)}) copy-start(bf16[96,2304]{1,0:T(8,128)(2,1)} %param.24) | copy-start | bytes 1327108
  6.5 46.0 %all-gather.3.cloned.1.call-start = ((), (), s32[]{:S(2)}) async-start(), calls=%async_computation | async-start | bytes 1880064 | tf_op jit(solution)/shard_map/all_gather | solution.py:82
  7.3 117.9 %all-gather.5.cloned.1.call-start = ((), (), s32[]{:S(2)}) async-start(), calls=%async_computation.1 | async-start | bytes 1880064 | tf_op jit(solution)/shard_map/all_gather | solution.py:105
  10.3 48.0 %copy-start.2 = (bf16[25,2304]{1,0:T(8,128)(2,1)S(1)}, bf16[25,2304]{1,0:T(8,128)(2,1)}, u32[]{:S(2)}) copy-start(bf16[25,2304]{1,0:T(8,128)(2,1)} %param.19) | copy-start | bytes 345604
  10.4 56.3 %copy-start.11 = (s32[16]{0:T(128)S(1)}, s32[16]{0:T(128)}, u32[]{:S(2)}) copy-start(s32[16]{0:T(128)} %param.29) | copy-start | bytes 196
  10.4 61.6 %copy-start.3 = (f32[2304]{0:T(1024)S(1)}, f32[2304]{0:T(1024)}, u32[]{:S(2)}) copy-start(f32[2304]{0:T(1024)} %param.18) | copy-start | bytes 27652
  10.4 61.6 %copy-start.4 = (f32[2304]{0:T(1024)S(1)}, f32[2304]{0:T(1024)}, u32[]{:S(2)}) copy-start(f32[2304]{0:T(1024)} %param.17) | copy-start | bytes 27652
  56.4 1.3 collective-permute-start
  57.7 4.0 %collective-permute-start.1 = (f32[2,2,2304]{2,1,0:T(2,128)S(1)}, f32[2,2,2304]{2,1,0:T(2,128)S(1)}, u32[]{:S(2)}, u32[]{:S(2)}) collective-permute-start(f32[2,2,2304]{2,1,0:T(2,128)S(1)} %fusion.25), channel_id=1, source_target_pairs={{0,2},{1,3},{2,0},{3,1},{4,6},{5,7},{6,4},{7,5},{8,10},{9,11},{10,... | collective-permute-start | bytes 110600 | tf_op jit(solution)/shard_map/ppermute | solution.py:17
  61.8 4.0 %collective-permute-start.2 = (f32[2,2,2304]{2,1,0:T(2,128)S(1)}, f32[2,2,2304]{2,1,0:T(2,128)S(1)}, u32[]{:S(2)}, u32[]{:S(2)}) collective-permute-start(f32[2,2,2304]{2,1,0:T(2,128)S(1)} %fusion.39), channel_id=1, source_target_pairs={{0,4},{1,5},{2,6},{3,7},{4,0},{5,1},{6,2},{7,3},{8,12},{9,13},{10,... | collective-permute-start | bytes 110600 | tf_op jit(solution)/shard_map/ppermute | solution.py:17
  65.9 5.9 %collective-permute-start.3 = (f32[2,2,2304]{2,1,0:T(2,128)S(1)}, f32[2,2,2304]{2,1,0:T(2,128)S(1)}, u32[]{:S(2)}, u32[]{:S(2)}) collective-permute-start(f32[2,2,2304]{2,1,0:T(2,128)S(1)} %add.186), channel_id=1, source_target_pairs={{0,8},{1,9},{2,10},{3,11},{4,12},{5,13},{6,14},{7,15},{8,0},{9,1},... | collective-permute-start | bytes 110600 | tf_op jit(solution)/shard_map/ppermute | solution.py:17
  108.3 14.8 %copy-start.5 = (f32[2304]{0:T(1024)S(1)}, f32[2304]{0:T(1024)}, u32[]{:S(2)}) copy-start(f32[2304]{0:T(1024)} %param.21) | copy-start | bytes 27652
  108.3 14.8 %copy-start.6 = (f32[2304]{0:T(1024)S(1)}, f32[2304]{0:T(1024)}, u32[]{:S(2)}) copy-start(f32[2304]{0:T(1024)} %param.20) | copy-start | bytes 27652
  108.4 1.3 collective-permute-start.4
  109.8 4.0 %collective-permute-start.5 = (f32[2,2,2304]{2,1,0:T(2,128)S(1)}, f32[2,2,2304]{2,1,0:T(2,128)S(1)}, u32[]{:S(2)}, u32[]{:S(2)}) collective-permute-start(f32[2,2,2304]{2,1,0:T(2,128)S(1)} %fusion.26), channel_id=1, source_target_pairs={{0,2},{1,3},{2,0},{3,1},{4,6},{5,7},{6,4},{7,5},{8,10},{9,11},{10,... | collective-permute-start | bytes 110600 | tf_op jit(solution)/shard_map/ppermute | solution.py:17
  113.9 4.0 %collective-permute-start.6 = (f32[2,2,2304]{2,1,0:T(2,128)S(1)}, f32[2,2,2304]{2,1,0:T(2,128)S(1)}, u32[]{:S(2)}, u32[]{:S(2)}) collective-permute-start(f32[2,2,2304]{2,1,0:T(2,128)S(1)} %fusion.38), channel_id=1, source_target_pairs={{0,4},{1,5},{2,6},{3,7},{4,0},{5,1},{6,2},{7,3},{8,12},{9,13},{10,... | collective-permute-start | bytes 110600 | tf_op jit(solution)/shard_map/ppermute | solution.py:17
  118.0 4.9 %collective-permute-start.7 = (f32[2,2,2304]{2,1,0:T(2,128)S(1)}, f32[2,2,2304]{2,1,0:T(2,128)S(1)}, u32[]{:S(2)}, u32[]{:S(2)}) collective-permute-start(f32[2,2,2304]{2,1,0:T(2,128)S(1)} %add.218), channel_id=1, source_target_pairs={{0,8},{1,9},{2,10},{3,11},{4,12},{5,13},{6,14},{7,15},{8,0},{9,1},... | collective-permute-start | bytes 110600 | tf_op jit(solution)/shard_map/ppermute | solution.py:17
  118.1 6.6 %copy-start.1 = (bf16[2304,96]{0,1:T(8,128)(2,1)S(1)}, bf16[2304,96]{0,1:T(8,128)(2,1)}, u32[]{:S(2)}) copy-start(bf16[2304,96]{0,1:T(8,128)(2,1)} %param.22) | copy-start | bytes 1327108
  118.1 6.6 %copy-start.10 = (f32[96]{0:T(128)S(1)}, f32[96]{0:T(128)}, u32[]{:S(2)}) copy-start(f32[96]{0:T(128)} %param.23) | copy-start | bytes 1156
  118.1 7.0 %copy-start.7 = (f32[2304]{0:T(1024)S(1)}, f32[2304]{0:T(1024)}, u32[]{:S(2)}) copy-start(f32[2304]{0:T(1024)} %param.25) | copy-start | bytes 27652
  125.1 17.3 %copy-start.8 = (f32[384]{0:T(512)S(1)}, f32[384]{0:T(512)}, u32[]{:S(2)}) copy-start(f32[384]{0:T(512)} %param.28) | copy-start | bytes 4612
  125.1 17.3 %copy-start.9 = (f32[384]{0:T(512)S(1)}, f32[384]{0:T(512)}, u32[]{:S(2)}) copy-start(f32[384]{0:T(512)} %param.27) | copy-start | bytes 4612
  129.2 1.2 collective-permute-start.8
  130.5 3.6 %collective-permute-start.9 = (f32[2,2,384]{2,1,0:T(2,128)S(1)}, f32[2,2,384]{2,1,0:T(2,128)S(1)}, u32[]{:S(2)}, u32[]{:S(2)}) collective-permute-start(f32[2,2,384]{2,1,0:T(2,128)S(1)} %fusion.24), channel_id=1, source_target_pairs={{0,2},{1,3},{2,0},{3,1},{4,6},{5,7},{6,4},{7,5},{8,10},{9,11},{10,... | collective-permute-start | bytes 18440 | tf_op jit(solution)/shard_map/ppermute | solution.py:17
  134.2 3.6 %collective-permute-start.10 = (f32[2,2,384]{2,1,0:T(2,128)S(1)}, f32[2,2,384]{2,1,0:T(2,128)S(1)}, u32[]{:S(2)}, u32[]{:S(2)}) collective-permute-start(f32[2,2,384]{2,1,0:T(2,128)S(1)} %fusion.37), channel_id=1, source_target_pairs={{0,4},{1,5},{2,6},{3,7},{4,0},{5,1},{6,2},{7,3},{8,12},{9,13},{10,... | collective-permute-start | bytes 18440 | tf_op jit(solution)/shard_map/ppermute | solution.py:17
  137.8 4.5 %collective-permute-start.11 = (f32[2,2,384]{2,1,0:T(2,128)S(1)}, f32[2,2,384]{2,1,0:T(2,128)S(1)}, u32[]{:S(2)}, u32[]{:S(2)}) collective-permute-start(f32[2,2,384]{2,1,0:T(2,128)S(1)} %add.233), channel_id=1, source_target_pairs={{0,8},{1,9},{2,10},{3,11},{4,12},{5,13},{6,14},{7,15},{8,0},{9,1},... | collective-permute-start | bytes 18440 | tf_op jit(solution)/shard_map/ppermute | solution.py:17
Sparse Core Ops, SparseCore 0:
  9.5 42.9 all-gather.2
  56.8 39.1 all-gather.4
